TPU v7x, 32 devices: a whole 2x2x4 slice. The times are simulated.
32 devices in a mesh: dp: 32 (over z, y, x, core).
Axes of the slice: x: 2, y: 2, z: 4, core: 2. Of those that a mesh axis runs over, the one named last changes fastest.
Arguments:
- grads: float32 [32, 1048576], P('dp')
- master: float32 [1048576], P('dp'), may hold values from -0.75 to 0.75
- m_old: float32 [32, 65536], P('dp'), may hold values from -6 to 6
- v_old: float32 [32, 65536], P('dp'), may hold values from 0.25 to 4
- old_bounds: int32 [33], replicated, may hold values from 0 to 1048576, as said below
Outputs:
- master_new: float32 [1048576], P('dp')
- m_new: float32 [1048576], P('dp')
- v_new: float32 [1048576], P('dp')
- params_full: bfloat16 [1048576], replicated
Inputs may be any that keep to these rules, and one draw needn't show every extreme that they name: old_bounds[0] = 0, the last entry is 1048576, entries never fall, and old_bounds[i] - i * 32768 lies between -16384 and 16384 for every i. Row k of m_old and v_old holds its span in its first old_bounds[k+1] - old_bounds[k] slots; later slots are unused. Some span has exactly 65536 entries in every draw.
All inputs are finite; a program needn't handle non-finite values.
Results may differ from a plain program's by a relative error of at most 0.0049.
Values may be sent and summed in bfloat16 or wider, within the bound.
A program may use at most 128 MiB of HBM per device.

v0:
```python
import jax
import jax.numpy as jnp
from jax import lax
from jax.sharding import PartitionSpec as P


def shifted(value, axis, steps):
    count = lax.axis_size(axis)
    leading, last = (max(0, -steps), min(count, count - steps))
    return lax.ppermute(value, axis, [(source, source + steps) for source in range(leading, last)])


def window(buffer, offset, width):
    padded = jnp.pad(buffer, ((0, 0), (2 * width, width)))
    return lax.dynamic_slice_in_dim(padded, offset + 2 * width, width, 1)


def local(grads, master, m_old, v_old, old_bounds):
    count = lax.axis_size("dp")
    device = lax.axis_index("dp")
    width = master.shape[0]
    local_grad = grads[0]
    blocks = local_grad.reshape(count, width)
    received = lax.all_to_all(
        blocks.astype(jnp.bfloat16), "dp", split_axis=0, concat_axis=0, tiled=True
    ).astype(blocks.dtype)
    gradient = jnp.sum(received, axis=0)
    total = lax.psum(jnp.sum(gradient * gradient), "dp")
    packed = jnp.stack([m_old[0], v_old[0]])
    from_before = shifted(packed.astype(jnp.bfloat16), "dp", 1).astype(packed.dtype)
    from_after = shifted(packed.astype(jnp.bfloat16), "dp", -1).astype(packed.dtype)
    start = device * width
    bound_before = old_bounds[jnp.maximum(device - 1, 0)]
    bound_here = old_bounds[device]
    bound_after = old_bounds[device + 1]
    part_before = window(from_before, start - bound_before, width)
    part_here = window(packed, start - bound_here, width)
    part_after = window(from_after, start - bound_after, width)
    positions = start + jnp.arange(width, dtype=jnp.int32)
    moments = jnp.where(
        positions[None, :] < bound_here,
        part_before,
        jnp.where(positions[None, :] >= bound_after, part_after, part_here),
    )
    m_prev = moments[0]
    v_prev = moments[1]
    clip = jnp.minimum(1.0, jnp.sqrt(jnp.float32(count * width)) / (jnp.sqrt(total) + 1e-06))
    clipped = clip * gradient
    m_new = 0.5 * m_prev + 0.5 * clipped
    v_new = 0.95 * v_prev + 0.05 * clipped * clipped
    direction = m_new / (1.0 - 0.5**20) / (jnp.sqrt(v_new / (1.0 - 0.95**20)) + 1e-08)
    master_new = master - 0.05 * (direction + 0.1 * master)
    params_full = lax.all_gather(master_new.astype(jnp.bfloat16), "dp", axis=0, tiled=True)
    return (master_new, m_new, v_new, params_full)


def solution(mesh):
    return jax.shard_map(
        local,
        mesh=mesh,
        in_specs=(P("dp", None), P("dp"), P("dp", None), P("dp", None), P()),
        out_specs=(P("dp"), P("dp"), P("dp"), P()),
        check_vma=False,
    )
```

profile of v0, /device:TPU:0, one launch (start us, length us, event | category | flops | bytes accessed | tf_op | source)
XLA Modules:
  0.0 216.4 jit_solution(121898063759179521)
XLA Ops:
  7.2 1.5 fusion.5
  8.7 1.3 collective-permute-start.1
  10.0 3.7 %collective-permute-start = (bf16[2,65536]{1,0:T(2,128)(2,1)S(1)}, bf16[2,65536]{1,0:T(2,128)(2,1)}, u32[]{:S(2)}, u32[]{:S(2)}) collective-permute-start(bf16[2,65536]{1,0:T(2,128)(2,1)S(1)} %fusion.5), channel_id=1, source_target_pairs={{0,1},{1,2},{2,3},{3,4},{4,5},{5,6},{6,7},{7,8},{8,9},{9,10},{10,1... | collective-permute-start | bytes 786440 | tf_op jit(solution)/shard_map/ppermute | solution.py:10
  13.7 7.7 %convert_element_type.31 = bf16[1,1048576]{1,0:T(2,128)(2,1)} convert(f32[1,1048576]{1,0:T(1,128)} %param.5) | non-fusion elementwise | flops 1048576 | bytes 6291456 | tf_op jit(solution)/shard_map/convert_element_type | solution.py:25
  21.4 0.5 broadcast.41
  21.9 13.2 %reduce.1 = bf16[32,32768]{1,0:T(8,128)(2,1)S(1)} reduce(bf16[32,1,32768]{2,1,0:T(2,128)(2,1)} %bitcast.6, bf16[]{:T(256)} %broadcast.41), dimensions={1}, to_apply=%bitcast.4.reduce_sub_computation | reduce | bytes 4194306 | tf_op jit(solution)/shard_map/convert_element_type | solution.py:25
  35.1 2.8 %reshape.34 = bf16[32,2,16384]{2,1,0:T(2,128)(2,1)} reshape(bf16[32,32768]{1,0:T(8,128)(2,1)S(1)} %reduce.1) | data formatting | bytes 4194304
  37.9 0.0 copy-start.3
  37.9 0.0 copy-start
  37.9 0.0 copy-start.1
  37.9 8.1 %all-to-all-start = ((bf16[32,2,16384]{2,1,0:T(2,128)(2,1)}), bf16[32,2,16384]{2,1,0:T(2,128)(2,1)S(1)}, u32[]{:S(2)}, u32[]{:S(2)}) async-start(bf16[32,2,16384]{2,1,0:T(2,128)(2,1)} %reshape.34), calls=%async_computation | async-start | bytes 4194304 | tf_op jit(solution)/shard_map/all_to_all | solution.py:24
  46.0 0.0 all-gather.2.cloned.1.call-start
  46.0 0.0 copy-done.3
  46.0 0.6 fusion.8
  48.6 0.0 copy-done
  48.6 0.0 copy-done.1
  48.6 0.5 pad_maximum_fusion
  49.1 1.3 fusion.3
  50.5 0.0 collective-permute-done.1
  50.5 0.0 collective-permute-done
  50.5 2.1 fusion.1
  52.6 42.1 %all-to-all-done = bf16[32,2,16384]{2,1,0:T(2,128)(2,1)S(1)} async-done(((bf16[32,2,16384]{2,1,0:T(2,128)(2,1)}), bf16[32,2,16384]{2,1,0:T(2,128)(2,1)S(1)}, u32[]{:S(2)}, u32[]{:S(2)}) %all-to-all-start) | async-done | bytes 2097184 | tf_op jit(solution)/shard_map/all_to_all | solution.py:24
  94.7 6.7 %reshape.35 = bf16[32,1,32768]{2,1,0:T(2,128)(2,1)} reshape(bf16[32,2,16384]{2,1,0:T(2,128)(2,1)S(1)} %all-to-all-done) | data formatting | bytes 4194304
  101.4 0.0 copy-start.2
  101.4 7.2 %convert_reduce_fusion = f32[32768]{0:T(1024)S(1)} fusion(bf16[32,1,32768]{2,1,0:T(2,128)(2,1)} %reshape.35), kind=kLoop, calls=%fused_computation | loop fusion | flops 2064384 | bytes 2228224 | tf_op jit(solution)/shard_map/reduce_sum | solution.py:27
  108.6 0.6 multiply_reduce_fusion
  109.3 0.2 slice_multiply_fusion
  109.5 38.4 %psum.7 = f32[]{:T(128)} all-reduce(f32[]{:T(128)} %multiply_reduce_fusion), channel_id=1, replica_groups=mesh['dp'=32] {'dp'}, use_global_device_ids=true, to_apply=%region_2.0 | all-reduce | flops 1 | bytes 8 | tf_op jit(solution)/shard_map/psum | solution.py:28
  148.6 0.0 copy-done.2
  148.6 0.9 fusion.6
  149.5 0.0 all-gather.2.cloned.1.call-update
  149.5 57.0 %all-gather.2.cloned.1.call-done = bf16[1048576]{0:T(1024)(128)(2,1)} async-done(((bf16[32768]{0:T(1024)(128)(2,1)}), bf16[1048576]{0:T(1024)(128)(2,1)}) %all-gather.2.cloned.1.call-update) | async-done | bytes 2097168 | tf_op jit(solution)/shard_map/all_gather | solution.py:53
  206.5 3.0 %copy.10 = bf16[1048576]{0:T(1024)(128)(2,1)} copy(bf16[1048576]{0:T(1024)(128)(2,1)} %all-gather.2.cloned.1.call-done) | data formatting | bytes 4194304
Async XLA Ops:
  8.7 41.8 %collective-permute-start.1 = (bf16[2,65536]{1,0:T(2,128)(2,1)S(1)}, bf16[2,65536]{1,0:T(2,128)(2,1)}, u32[]{:S(2)}, u32[]{:S(2)}) collective-permute-start(bf16[2,65536]{1,0:T(2,128)(2,1)S(1)} %fusion.5), channel_id=1, source_target_pairs={{1,0},{2,1},{3,2},{4,3},{5,4},{6,5},{7,6},{8,7},{9,8},{10,9},{11,1... | collective-permute-start | bytes 786440 | tf_op jit(solution)/shard_map/ppermute | solution.py:10
  10.0 40.5 %collective-permute-start = (bf16[2,65536]{1,0:T(2,128)(2,1)S(1)}, bf16[2,65536]{1,0:T(2,128)(2,1)}, u32[]{:S(2)}, u32[]{:S(2)}) collective-permute-start(bf16[2,65536]{1,0:T(2,128)(2,1)S(1)} %fusion.5), channel_id=1, source_target_pairs={{0,1},{1,2},{2,3},{3,4},{4,5},{5,6},{6,7},{7,8},{8,9},{9,10},{10,1... | collective-permute-start | bytes 786440 | tf_op jit(solution)/shard_map/ppermute | solution.py:10
  37.9 8.2 %copy-start.3 = (s32[33]{0:T(128)S(1)}, s32[33]{0:T(128)}, u32[]{:S(2)}) copy-start(s32[33]{0:T(128)} %param.9) | copy-start | bytes 400
  37.9 10.7 %copy-start = (f32[1,65536]{1,0:T(1,128)S(1)}, f32[1,65536]{1,0:T(1,128)}, u32[]{:S(2)}) copy-start(f32[1,65536]{1,0:T(1,128)} %param.8) | copy-start | bytes 786436
  37.9 10.7 %copy-start.1 = (f32[1,65536]{1,0:T(1,128)S(1)}, f32[1,65536]{1,0:T(1,128)}, u32[]{:S(2)}) copy-start(f32[1,65536]{1,0:T(1,128)} %param.7) | copy-start | bytes 786436
  37.9 56.8 %all-to-all-start = ((bf16[32,2,16384]{2,1,0:T(2,128)(2,1)}), bf16[32,2,16384]{2,1,0:T(2,128)(2,1)S(1)}, u32[]{:S(2)}, u32[]{:S(2)}) async-start(bf16[32,2,16384]{2,1,0:T(2,128)(2,1)} %reshape.34), calls=%async_computation | async-start | bytes 4194304 | tf_op jit(solution)/shard_map/all_to_all | solution.py:24
  46.0 160.5 %all-gather.2.cloned.1.call-start = ((), (), s32[]{:S(2)}) async-start(), calls=%async_computation.1 | async-start | bytes 2162688 | tf_op jit(solution)/shard_map/all_gather | solution.py:53
  101.4 47.2 %copy-start.2 = (f32[32768]{0:T(1024)S(1)}, f32[32768]{0:T(1024)}, u32[]{:S(2)}) copy-start(f32[32768]{0:T(1024)} %param.6) | copy-start | bytes 393220
Sparse Core Ops, SparseCore 0:
  149.6 56.7 all-gather.1
where the time goes:
time: 217 us; the launch traced here: 216 us
  waiting for transfers between devices  99.1 us (46%)
  blocking collectives  38.4 us (18%)
  other arithmetic  35.2 us (16%)
  between operations  16.9 us (8%)
  local copies, waits for them, and re-layouts  13.7 us (6%)
  starting transfers between devices  13.2 us (6%)
    all_gather x1, waiting for transfers between devices, local(): lax.all_gather(master_new.astype(jnp.bfloat16), 'dp', axis=0, tiled=True)  57 us
    all_to_all x1, waiting for transfers between devices, local(): lax.all_to_all(blocks.astype(jnp.bfloat16), 'dp', split_axis=0, concat_ax...  42.1 us
    psum x1, blocking collectives, local(): total = lax.psum(jnp.sum(gradient * gradient), 'dp')  38.4 us
    convert_element_type x2, other arithmetic, local(): blocks.astype(jnp.bfloat16)  20.8 us
    unnamed x11, local copies, waits for them, and re-layouts  12.6 us
    all_to_all x1, starting transfers between devices, local(): lax.all_to_all(blocks.astype(jnp.bfloat16), 'dp', split_axis=0, concat_ax...  8.1 us
    reduce_sum x1, other arithmetic, local(): gradient = jnp.sum(received, axis=0)  7.19 us
    ppermute x2, starting transfers between devices, shifted(): lax.ppermute(value, axis, [(source, source + steps) for source in range(l...  5.03 us
  transfers between devices with their start and end apart: 4, of which 2 were waited for; matrix products, arithmetic and copies ran while one was open for 13% of the time, Pallas kernels for 0%

commit v1 on v0

v1 whole, which is shorter than its diff:
```python
import functools

import jax
import jax.numpy as jnp
from jax import lax
from jax.experimental import pallas as pl
from jax.experimental.pallas import tpu as pltpu
from jax.sharding import PartitionSpec as P

MESH = pl.DeviceIdType.MESH
LANES = 128
F32 = jnp.float32
BF16 = jnp.bfloat16


def grid_of(count):
    sizes, chips, turn = [1, 1, 1], count // 2, 0
    while chips > 1:
        sizes[turn % 3] *= 2
        chips //= 2
        turn += 1
    return tuple(sizes)


def kernel(
    dims, grads, master, m_old, v_old, bounds,
    master_out, m_out, v_out, full,
    own_a, own_b, mate_a, mate_b,
    send_a1, send_b1, recv_a1, recv_b1,
    send_a2, send_b2, recv_a2, recv_b2, keep_a, keep_b,
    send_z, recv_z, gradient,
    spans, here, edge_out, edge_in, prev, weights, norm_out, norm_in,
    load_sem, own_sem_a, own_sem_b,
    mate_ss_a, mate_rs_a, mate_ss_b, mate_rs_b,
    ss_a1, rs_a1, ss_b1, rs_b1, ss_a2, rs_a2, ss_b2, rs_b2, ss_z, rs_z,
    edge_ss, edge_rs, norm_ss, norm_rs,
    gz_ss, gz_rs, gx_ss, gx_rs, gy_ss, gy_rs, gxy_ss, gxy_rs, gyx_ss, gyx_rs,
    d_ss, d_rs, dx_ss, dx_rs, dy_ss, dy_rs, dxy_ss, dxy_rs, dyx_ss, dyx_rs,
):
    Z, Y, X = dims
    count = Z * Y * X * 2
    rows = master.shape[0]
    half = rows // 2
    me = lax.axis_index("dp")
    core = me % 2
    x = (me // 2) % X
    y = (me // (2 * X)) % Y
    z = me // (2 * X * Y)

    def device(zz, yy, xx, cc):
        return ((zz * Y + yy) * X + xx) * 2 + cc

    mate = device(z, y, x, 1 - core)

    def at(coord, step, size):
        return (coord + step) % size

    sends = []

    def send(src, dst, ss, rs, target):
        copy = pltpu.make_async_remote_copy(
            src_ref=src, dst_ref=dst, send_sem=ss, recv_sem=rs,
            device_id=(target,), device_id_type=MESH)
        copy.start()
        sends.append(copy)

    def arrived(dst, ss, rs):
        pltpu.make_async_remote_copy(
            src_ref=dst, dst_ref=dst, send_sem=ss, recv_sem=rs,
            device_id=(mate,), device_id_type=MESH).wait_recv()

    barrier = pltpu.get_barrier_semaphore()

    @pl.loop(1, count)
    def _(step):
        pl.semaphore_signal(barrier, inc=1, device_id=((me + step) % count,), device_id_type=MESH)

    pad = rows + 8
    load_m = pltpu.make_async_copy(m_old, spans.at[0, pl.ds(pad, 2 * rows)], load_sem.at[0])
    load_v = pltpu.make_async_copy(v_old, spans.at[1, pl.ds(pad, 2 * rows)], load_sem.at[1])
    load_w = pltpu.make_async_copy(master, weights, load_sem.at[2])
    load_m.start()
    load_v.start()
    order = [s for s in sorted(range(1, Z), key=lambda s: abs(s - Z / 2))] + [0]
    first, second = slice(0, half), slice(half, rows)
    loads_a, loads_b = {}, {}
    for s in order:
        for o in list(range(1, X)) + [0]:
            loads_a[o, s] = pltpu.make_async_copy(
                grads.at[at(z, s, Z), :, at(x, o, X), core, pl.ds(0, half)],
                own_a.at[o, s], own_sem_a.at[o, s])
            loads_a[o, s].start()
        for o in list(range(1, Y)) + [0]:
            loads_b[o, s] = pltpu.make_async_copy(
                grads.at[at(z, s, Z), at(y, o, Y), :, core, pl.ds(half, half)],
                own_b.at[o, s], own_sem_b.at[o, s])
            loads_b[o, s].start()
    load_w.start()

    here_bound = bounds[me] - me * (rows * LANES)
    next_bound = bounds[me + 1] - me * (rows * LANES)
    shift = jnp.clip(here_bound + half * LANES, 0, rows * LANES)
    lift, turn = shift // LANES, shift % LANES
    spans[:, pl.ds(0, pad)] = jnp.zeros((2, pad, LANES), F32)
    load_m.wait()
    load_v.wait()
    tile = 32
    lane = lax.broadcasted_iota(jnp.int32, (tile, LANES), 1)

    def aligned(which, row):
        base = pad + row - lift
        now = pltpu.roll(spans[which, pl.ds(base, tile)], turn, 1)
        before = pltpu.roll(spans[which, pl.ds(base - 1, tile)], turn, 1)
        return jnp.where(lane >= turn, now, before)

    for which in range(2):
        @pl.loop(0, half // tile)
        def _(i, which=which):
            row = pl.multiple_of(i * tile, tile)
            edge_out[0, which, pl.ds(row, tile)] = aligned(which, row).astype(BF16)
            edge_out[1, which, pl.ds(row, tile)] = aligned(which, row + 3 * half).astype(BF16)
            here[which, pl.ds(row, tile)] = aligned(which, row + half)
            here[which, pl.ds(row + half, tile)] = aligned(which, row + 2 * half)

    pl.semaphore_wait(barrier, count - 1)

    for s in order:
        for o in list(range(1, X)) + [0]:
            send(grads.at[at(z, s, Z), :, at(x, o, X), 1 - core, pl.ds(0, half)],
                 mate_a.at[o, s], mate_ss_a.at[o, s], mate_rs_a.at[o, s], mate)
        for o in list(range(1, Y)) + [0]:
            send(grads.at[at(z, s, Z), at(y, o, Y), :, 1 - core, pl.ds(half, half)],
                 mate_b.at[o, s], mate_ss_b.at[o, s], mate_rs_b.at[o, s], mate)

    def chip_ready_a(o, s):
        loads_a[o, s].wait()
        arrived(mate_a.at[o, s], mate_ss_a.at[o, s], mate_rs_a.at[o, s])

    def chip_ready_b(o, s):
        loads_b[o, s].wait()
        arrived(mate_b.at[o, s], mate_ss_b.at[o, s], mate_rs_b.at[o, s])

    def exchange_one(s):
        for o in range(1, X):
            chip_ready_a(o, s)
            for j in range(Y):
                send_a1[o - 1, s, j] = (own_a[o, s, j] + mate_a[o, s, j]).astype(BF16)
            send(send_a1.at[o - 1, s], recv_a1.at[o - 1, s], ss_a1.at[o - 1, s], rs_a1.at[o - 1, s],
                 device(z, y, at(x, o, X), core))
        for o in range(1, Y):
            chip_ready_b(o, s)
            for j in range(X):
                send_b1[o - 1, s, j] = (own_b[o, s, j] + mate_b[o, s, j]).astype(BF16)
            send(send_b1.at[o - 1, s], recv_b1.at[o - 1, s], ss_b1.at[o - 1, s], rs_b1.at[o - 1, s],
                 device(z, at(y, o, Y), x, core))

    def exchange_two(s):
        chip_ready_a(0, s)
        for o in range(1, X):
            arrived(recv_a1.at[o - 1, s], ss_a1.at[o - 1, s], rs_a1.at[o - 1, s])

        def sum_a(j):
            value = own_a[0, s, j] + mate_a[0, s, j]
            for o in range(1, X):
                value = value + recv_a1[o - 1, s, j].astype(F32)
            return value

        for o in range(1, Y):
            send_a2[o - 1, s] = sum_a(at(y, o, Y)).astype(BF16)
            send(send_a2.at[o - 1, s], recv_a2.at[o - 1, s], ss_a2.at[o - 1, s], rs_a2.at[o - 1, s],
                 device(z, at(y, o, Y), x, core))
        keep_a[s] = sum_a(y)
        chip_ready_b(0, s)
        for o in range(1, Y):
            arrived(recv_b1.at[o - 1, s], ss_b1.at[o - 1, s], rs_b1.at[o - 1, s])

        def sum_b(j):
            value = own_b[0, s, j] + mate_b[0, s, j]
            for o in range(1, Y):
                value = value + recv_b1[o - 1, s, j].astype(F32)
            return value

        for o in range(1, X):
            send_b2[o - 1, s] = sum_b(at(x, o, X)).astype(BF16)
            send(send_b2.at[o - 1, s], recv_b2.at[o - 1, s], ss_b2.at[o - 1, s], rs_b2.at[o - 1, s],
                 device(z, y, at(x, o, X), core))
        keep_b[s] = sum_b(x)

    def exchange_three(s):
        for o in range(1, Y):
            arrived(recv_a2.at[o - 1, s], ss_a2.at[o - 1, s], rs_a2.at[o - 1, s])
        value_a = keep_a[s]
        for o in range(1, Y):
            value_a = value_a + recv_a2[o - 1, s].astype(F32)
        for o in range(1, X):
            arrived(recv_b2.at[o - 1, s], ss_b2.at[o - 1, s], rs_b2.at[o - 1, s])
        value_b = keep_b[s]
        for o in range(1, X):
            value_b = value_b + recv_b2[o - 1, s].astype(F32)
        if s == 0:
            gradient[pl.ds(0, half)] = value_a
            gradient[pl.ds(half, half)] = value_b
        else:
            send_z[s - 1, pl.ds(0, half)] = value_a.astype(BF16)
            send_z[s - 1, pl.ds(half, half)] = value_b.astype(BF16)
            send(send_z.at[s - 1], recv_z.at[s - 1], ss_z.at[s - 1], rs_z.at[s - 1],
                 device(at(z, s, Z), y, x, core))

    for s in order:
        exchange_one(s)
    send(edge_out.at[0], edge_in.at[0], edge_ss.at[0], edge_rs.at[0], (me + count - 1) % count)
    send(edge_out.at[1], edge_in.at[1], edge_ss.at[1], edge_rs.at[1], (me + 1) % count)
    for i in range(Z + 1):
        if i < Z:
            exchange_two(order[i])
        if i > 0:
            exchange_three(order[i - 1])
    for s in order[:-1]:
        arrived(recv_z.at[s - 1], ss_z.at[s - 1], rs_z.at[s - 1])

    squares = jnp.zeros((8, LANES), F32)
    for i in range(rows // tile):
        part = gradient[pl.ds(i * tile, tile)]
        for s in order[:-1]:
            part = part + recv_z[s - 1, pl.ds(i * tile, tile)].astype(F32)
        gradient[pl.ds(i * tile, tile)] = part
        squares = squares + jnp.sum((part * part).reshape(tile // 8, 8, LANES), axis=0)
    mine = jnp.sum(squares, axis=0, keepdims=True)
    norm_out[...] = mine
    norm_in[me] = mine

    @pl.loop(1, count)
    def _(step):
        pltpu.make_async_remote_copy(
            src_ref=norm_out, dst_ref=norm_in.at[me], send_sem=norm_ss.at[step], recv_sem=norm_rs.at[me],
            device_id=((me + step) % count,), device_id_type=MESH).start()

    for e in range(2):
        arrived(edge_in.at[e], edge_ss.at[e], edge_rs.at[e])
    place = lax.broadcasted_iota(jnp.int32, (tile, LANES), 0) * LANES + lane

    @pl.loop(0, half // tile)
    def _(i):
        row = pl.multiple_of(i * tile, tile)
        low = row * LANES + place
        high = low + half * LANES
        for which in range(2):
            prev[which, pl.ds(row, tile)] = jnp.where(
                low < here_bound, edge_in[1, which, pl.ds(row, tile)].astype(F32),
                here[which, pl.ds(row, tile)])
            prev[which, pl.ds(row + half, tile)] = jnp.where(
                high >= next_bound, edge_in[0, which, pl.ds(row, tile)].astype(F32),
                here[which, pl.ds(row + half, tile)])

    load_w.wait()

    @pl.loop(1, count)
    def _(step):
        other = (me + step) % count
        pltpu.make_async_remote_copy(
            src_ref=norm_out, dst_ref=norm_in.at[other], send_sem=norm_ss.at[step], recv_sem=norm_rs.at[other],
            device_id=(other,), device_id_type=MESH).wait()

    total = jnp.sum(jnp.sum(norm_in[...], axis=0), axis=1, keepdims=True)
    size = jnp.float32(count * rows * LANES)
    clip = jnp.minimum(1.0, jnp.sqrt(size) / (jnp.sqrt(total) + 1e-06))

    for i in range(rows // tile):
        part = pl.ds(i * tile, tile)
        clipped = clip * gradient[part]
        m_new = 0.5 * prev[0, part] + 0.5 * clipped
        v_new = 0.95 * prev[1, part] + 0.05 * clipped * clipped
        direction = m_new / (1.0 - 0.5**20) / (jnp.sqrt(v_new / (1.0 - 0.95**20)) + 1e-08)
        weight = weights[part]
        weight = weight - 0.05 * (direction + 0.1 * weight)
        full[z, y, x, core, part] = weight.astype(BF16)
        master_out[part] = weight
        m_out[part] = m_new
        v_out[part] = v_new

    lower, upper = pl.ds(0, half), pl.ds(half, half)

    def spread(s):
        zz = at(z, Z - s, Z)
        block = full.at[zz, y, x, core]
        if s > 0:
            arrived(block, gz_ss.at[s - 1], gz_rs.at[s - 1])
        for o in range(1, X):
            send(block, block, gx_ss.at[o - 1, s], gx_rs.at[o - 1, s], device(z, y, at(x, o, X), core))
        for o in range(1, Y):
            send(block, block, gy_ss.at[o - 1, s], gy_rs.at[o - 1, s], device(z, at(y, o, Y), x, core))
        send(block, block, d_ss.at[s], d_rs.at[s], mate)

    def turn_corner(s):
        zz = at(z, Z - s, Z)
        for o in range(1, X):
            block = full.at[zz, y, at(x, X - o, X), core]
            arrived(block, gx_ss.at[o - 1, s], gx_rs.at[o - 1, s])
            for p in range(1, Y):
                send(block.at[lower], block.at[lower], gxy_ss.at[o - 1, p - 1, s], gxy_rs.at[o - 1, p - 1, s],
                     device(z, at(y, p, Y), x, core))
            send(block, block, dx_ss.at[o - 1, s], dx_rs.at[o - 1, s], mate)
        for p in range(1, Y):
            block = full.at[zz, at(y, Y - p, Y), x, core]
            arrived(block, gy_ss.at[p - 1, s], gy_rs.at[p - 1, s])
            for o in range(1, X):
                send(block.at[upper], block.at[upper], gyx_ss.at[o - 1, p - 1, s], gyx_rs.at[o - 1, p - 1, s],
                     device(z, y, at(x, o, X), core))
            send(block, block, dy_ss.at[p - 1, s], dy_rs.at[p - 1, s], mate)

    def finish(s):
        zz = at(z, Z - s, Z)
        for o in range(1, X):
            for p in range(1, Y):
                block = full.at[zz, at(y, Y - p, Y), at(x, X - o, X), core]
                index = (o - 1, p - 1, s)
                arrived(block.at[lower], gxy_ss.at[index], gxy_rs.at[index])
                send(block.at[lower], block.at[lower], dxy_ss.at[index], dxy_rs.at[index], mate)
                arrived(block.at[upper], gyx_ss.at[index], gyx_rs.at[index])
                send(block.at[upper], block.at[upper], dyx_ss.at[index], dyx_rs.at[index], mate)

    mine = full.at[z, y, x, core]
    for s in order[:-1]:
        send(mine, mine, gz_ss.at[s - 1], gz_rs.at[s - 1], device(at(z, s, Z), y, x, core))
    ring = [0] + sorted(range(1, Z), key=lambda s: -abs(s - Z / 2))
    for i in range(Z + 2):
        if i < Z:
            spread(ring[i])
        if 0 <= i - 1 < Z:
            turn_corner(ring[i - 1])
        if 0 <= i - 2 < Z:
            finish(ring[i - 2])
    for s in range(Z):
        zz = at(z, Z - s, Z)
        arrived(full.at[zz, y, x, 1 - core], d_ss.at[s], d_rs.at[s])
        for o in range(1, X):
            arrived(full.at[zz, y, at(x, X - o, X), 1 - core], dx_ss.at[o - 1, s], dx_rs.at[o - 1, s])
        for p in range(1, Y):
            arrived(full.at[zz, at(y, Y - p, Y), x, 1 - core], dy_ss.at[p - 1, s], dy_rs.at[p - 1, s])
            for o in range(1, X):
                block = full.at[zz, at(y, Y - p, Y), at(x, X - o, X), 1 - core]
                index = (o - 1, p - 1, s)
                arrived(block.at[lower], dxy_ss.at[index], dxy_rs.at[index])
                arrived(block.at[upper], dyx_ss.at[index], dyx_rs.at[index])
    for copy in sends:
        copy.wait_send()


def local(dims, grads, master, m_old, v_old, old_bounds):
    Z, Y, X = dims
    count = Z * Y * X * 2
    width = master.shape[0]
    rows = width // LANES
    half = rows // 2
    dma = pltpu.SemaphoreType.DMA
    two = lambda *shape: [dma(shape), dma(shape)]
    vmem = pltpu.VMEM
    anywhere = pl.BlockSpec(memory_space=pl.ANY)
    inside = pl.BlockSpec(memory_space=pltpu.VMEM)
    scratch = [
        vmem((X, Z, Y, half, LANES), F32), vmem((Y, Z, X, half, LANES), F32),
        vmem((X, Z, Y, half, LANES), F32), vmem((Y, Z, X, half, LANES), F32),
        vmem((X - 1, Z, Y, half, LANES), BF16), vmem((Y - 1, Z, X, half, LANES), BF16),
        vmem((X - 1, Z, Y, half, LANES), BF16), vmem((Y - 1, Z, X, half, LANES), BF16),
        vmem((Y - 1, Z, half, LANES), BF16), vmem((X - 1, Z, half, LANES), BF16),
        vmem((Y - 1, Z, half, LANES), BF16), vmem((X - 1, Z, half, LANES), BF16),
        vmem((Z, half, LANES), F32), vmem((Z, half, LANES), F32),
        vmem((Z - 1, rows, LANES), BF16), vmem((Z - 1, rows, LANES), BF16),
        vmem((rows, LANES), F32),
        vmem((2, 3 * rows + 8, LANES), F32), vmem((2, rows, LANES), F32),
        vmem((2, 2, half, LANES), BF16), vmem((2, 2, half, LANES), BF16),
        vmem((2, rows, LANES), F32), vmem((rows, LANES), F32),
        vmem((1, LANES), F32), vmem((count, 1, LANES), F32),
        dma((3,)), dma((X, Z)), dma((Y, Z)),
        *two(X, Z), *two(Y, Z),
        *two(X - 1, Z), *two(Y - 1, Z), *two(Y - 1, Z), *two(X - 1, Z), *two(Z - 1),
        *two(2), *two(count),
        *two(Z - 1), *two(X - 1, Z), *two(Y - 1, Z), *two(X - 1, Y - 1, Z), *two(X - 1, Y - 1, Z),
        *two(Z), *two(X - 1, Z), *two(Y - 1, Z), *two(X - 1, Y - 1, Z), *two(X - 1, Y - 1, Z),
    ]
    flat = jax.ShapeDtypeStruct((rows, LANES), F32)
    master_new, m_new, v_new, full = pl.pallas_call(
        functools.partial(kernel, dims),
        out_shape=(flat, flat, flat, jax.ShapeDtypeStruct((Z, Y, X, 2, rows, LANES), BF16)),
        in_specs=[anywhere] * 4 + [pl.BlockSpec(memory_space=pltpu.SMEM)],
        out_specs=(inside,) * 4,
        scratch_shapes=scratch,
        compiler_params=pltpu.CompilerParams(
            collective_id=0, has_side_effects=True, vmem_limit_bytes=60 * 1024 * 1024),
    )(
        grads.reshape(Z, Y, X, 2, rows, LANES),
        master.reshape(rows, LANES),
        m_old.reshape(2 * rows, LANES),
        v_old.reshape(2 * rows, LANES),
        old_bounds,
    )
    return (master_new.reshape(width), m_new.reshape(width), v_new.reshape(width), full.reshape(count * width))


def solution(mesh):
    dims = grid_of(mesh.shape["dp"])
    return jax.shard_map(
        functools.partial(local, dims),
        mesh=mesh,
        in_specs=(P("dp", None), P("dp"), P("dp", None), P("dp", None), P()),
        out_specs=(P("dp"), P("dp"), P("dp"), P()),
        check_vma=False,
    )
```

time: 217 us -> 61.2 us (0.28)
  waiting for transfers between devices: 99.1 us -> 0 us
  Pallas kernels: 0 us -> 52.6 us
  blocking collectives: 38.4 us -> 0 us
  other arithmetic: 35.2 us -> 0 us
  between operations: 16.9 us -> 0.64 us
  starting transfers between devices: 13.2 us -> 0 us
  local copies, waits for them, and re-layouts: 13.7 us -> 7.75 us
    all_gather x1 -> x0, waiting for transfers between devices: 57 us -> none  [local(): lax.all_gather(master_new.astype(jnp.bfloat16), 'dp', axis=0, tiled=True)]
    pallas_call x0 -> x1, Pallas kernels: none -> 52.6 us  [local(): pl.pallas_call(functools.partial(kernel, dims), out_shape=(flat, flat, fl...]
    all_to_all x1 -> x0, waiting for transfers between devices: 42.1 us -> none  [local(): lax.all_to_all(blocks.astype(jnp.bfloat16), 'dp', split_axis=0, concat_ax...]
    psum x1 -> x0, blocking collectives: 38.4 us -> none  [local(): total = lax.psum(jnp.sum(gradient * gradient), 'dp')]
    convert_element_type x4 -> x0, other arithmetic: 23.2 us -> none  [the longest x2 20.8 us: local(): blocks.astype(jnp.bfloat16)]
    all_to_all x1 -> x0, starting transfers between devices: 8.1 us -> none  [local(): lax.all_to_all(blocks.astype(jnp.bfloat16), 'dp', split_axis=0, concat_ax...]
    reduce_sum x2 -> x0, other arithmetic: 7.82 us -> none  [the longest x1 7.19 us: local(): gradient = jnp.sum(received, axis=0)]
    ppermute x2 -> x0, starting transfers between devices: 5.03 us -> none  [shifted(): lax.ppermute(value, axis, [(source, source + steps) for source in range(l...]
  transfers between devices with their start and end apart: 4 -> 0, of which waited for: 2 -> 0; matrix products, arithmetic and copies ran while one was open for 13% -> 0% of each run, Pallas kernels for 0% -> 0%
where the time goes in v1:
time: 61.2 us; the launch traced here: 61 us
  Pallas kernels  52.6 us (86%)
  local copies, waits for them, and re-layouts  7.75 us (13%)
  between operations  0.64 us (1%)
    pallas_call x1, Pallas kernels, local(): pl.pallas_call(functools.partial(kernel, dims), out_shape=(flat, flat, fl...  52.6 us
    unnamed x4, local copies, waits for them, and re-layouts  7.75 us

profile of v1, /device:TPU:0, one launch (start us, length us, event | category | flops | bytes accessed | tf_op | source)
XLA Modules:
  0.0 61.0 jit_solution(16034220695501252476)
XLA Ops:
  0.6 52.6 %shard_map.84 = (f32[256,128]{1,0:T(8,128)}, f32[256,128]{1,0:T(8,128)}, f32[256,128]{1,0:T(8,128)}, bf16[4,2,2,2,256,128]{5,4,3,2,1,0:T(8,128)(2,1)}) custom-call(f32[4,2,2,2,256,128]{5,4,3,2,1,0:T(8,128)} %bitcast.8, f32[256,128]{1,0:T(8,128)} %bitcast.12, f32[512,128]{1,0:T(8,128)} %bitcast.10, f32[512,128]{1,0:T(8,128)} %bitcast.11, s32[33]{0:T(128)} %bounds.1), custom_call_target="tpu_custom_call" | custom-call | tf_op jit(solution)/shard_map/pallas_call | solution.py:382
  53.3 1.6 %copy.13 = f32[32768]{0:T(1024)} copy(f32[32768]{0:T(1024)} %bitcast.15) | data formatting | bytes 262144
  54.8 1.6 %copy.14 = f32[32768]{0:T(1024)} copy(f32[32768]{0:T(1024)} %bitcast.14) | data formatting | bytes 262144
  56.4 1.6 %copy.15 = f32[32768]{0:T(1024)} copy(f32[32768]{0:T(1024)} %bitcast.13) | data formatting | bytes 262144
  58.0 3.0 %copy.16 = bf16[1048576]{0:T(1024)(128)(2,1)} copy(bf16[1048576]{0:T(1024)(128)(2,1)} %bitcast.9) | data formatting | bytes 4194304

commit v2 on v1

--- a/solution.py
+++ b/solution.py
@@ -9,6 +9,7 @@
 
 MESH = pl.DeviceIdType.MESH
 LANES = 128
+VMEM_BYTES = 127 * 512 * 1024
 F32 = jnp.float32
 BF16 = jnp.bfloat16
 
@@ -355,7 +356,7 @@
     dma = pltpu.SemaphoreType.DMA
     two = lambda *shape: [dma(shape), dma(shape)]
     vmem = pltpu.VMEM
-    anywhere = pl.BlockSpec(memory_space=pl.ANY)
+    outside = pl.BlockSpec(memory_space=pltpu.HBM)
     inside = pl.BlockSpec(memory_space=pltpu.VMEM)
     scratch = [
         vmem((X, Z, Y, half, LANES), F32), vmem((Y, Z, X, half, LANES), F32),
@@ -378,15 +379,16 @@
         *two(Z - 1), *two(X - 1, Z), *two(Y - 1, Z), *two(X - 1, Y - 1, Z), *two(X - 1, Y - 1, Z),
         *two(Z), *two(X - 1, Z), *two(Y - 1, Z), *two(X - 1, Y - 1, Z), *two(X - 1, Y - 1, Z),
     ]
+    results = 12 * width + 2 * count * width
     flat = jax.ShapeDtypeStruct((rows, LANES), F32)
     master_new, m_new, v_new, full = pl.pallas_call(
         functools.partial(kernel, dims),
-        out_shape=(flat, flat, flat, jax.ShapeDtypeStruct((Z, Y, X, 2, rows, LANES), BF16)),
-        in_specs=[anywhere] * 4 + [pl.BlockSpec(memory_space=pltpu.SMEM)],
+        out_shape=(pltpu.VMEM((rows, LANES), F32),) * 3 + (pltpu.VMEM((Z, Y, X, 2, rows, LANES), BF16),),
+        in_specs=[outside] * 4 + [pl.BlockSpec(memory_space=pltpu.SMEM)],
         out_specs=(inside,) * 4,
         scratch_shapes=scratch,
         compiler_params=pltpu.CompilerParams(
-            collective_id=0, has_side_effects=True, vmem_limit_bytes=60 * 1024 * 1024),
+            collective_id=0, has_side_effects=True, vmem_limit_bytes=VMEM_BYTES - results),
     )(
         grads.reshape(Z, Y, X, 2, rows, LANES),
         master.reshape(rows, LANES),
@@ -394,6 +396,24 @@
         v_old.reshape(2 * rows, LANES),
         old_bounds,
     )
+
+    def publish(*refs):
+        ins, outs, sem = refs[:4], refs[4:8], refs[8]
+        copies = [pltpu.make_async_copy(i, o, sem.at[k]) for k, (i, o) in enumerate(zip(ins, outs))]
+        for c in copies:
+            c.start()
+        for c in copies:
+            c.wait()
+
+    master_new, m_new, v_new, full = [pltpu.with_memory_space_constraint(t, pltpu.VMEM) for t in (master_new, m_new, v_new, full)]
+    master_new, m_new, v_new, full = pl.pallas_call(
+        publish,
+        out_shape=(flat, flat, flat, jax.ShapeDtypeStruct((Z, Y, X, 2, rows, LANES), BF16)),
+        in_specs=[inside] * 4,
+        out_specs=(outside,) * 4,
+        scratch_shapes=[dma((4,))],
+        compiler_params=pltpu.CompilerParams(vmem_limit_bytes=1024 * 1024),
+    )(master_new, m_new, v_new, full)
     return (master_new.reshape(width), m_new.reshape(width), v_new.reshape(width), full.reshape(count * width))
 
 

time: 61.2 us -> 53.4 us (0.87)
  local copies, waits for them, and re-layouts: 7.75 us -> 0 us
    unnamed x4 -> x0, local copies, waits for them, and re-layouts: 7.75 us -> none
    pallas_call x1 -> x2, Pallas kernels: 52.6 us -> 52.6 us  [the longest x1 51.1 us: local(): pl.pallas_call(functools.partial(kernel, dims), out_shape=(pltpu.VMEM((ro...]
where the time goes in v2:
time: 53.4 us; the launch traced here: 53.3 us
  Pallas kernels  52.6 us (99%)
  between operations  0.64 us (1%)
    pallas_call x1, Pallas kernels, local(): pl.pallas_call(functools.partial(kernel, dims), out_shape=(pltpu.VMEM((ro...  51.1 us
    pallas_call x1, Pallas kernels, local(): pl.pallas_call(publish, out_shape=(flat, flat, flat, jax.ShapeDtypeStruct...  1.49 us

profile of v2, /device:TPU:0, one launch (start us, length us, event | category | flops | bytes accessed | tf_op | source)
XLA Modules:
  0.0 53.3 jit_solution(16152013156910167240)
XLA Ops:
  0.6 51.1 %shard_map.84 = (f32[256,128]{1,0:T(8,128)S(1)}, f32[256,128]{1,0:T(8,128)S(1)}, f32[256,128]{1,0:T(8,128)S(1)}, bf16[4,2,2,2,256,128]{5,4,3,2,1,0:T(8,128)(2,1)S(1)}) custom-call(f32[4,2,2,2,256,128]{5,4,3,2,1,0:T(8,128)} %bitcast.8, f32[256,128]{1,0:T(8,128)} %bitcast.11, f32[512,128]{1,0:T(8,128)} %bitcast.9, f32[512,128]{1,0:T(8,128)} %bitcast.10, s32[33]{0:T(128)} %bounds.1), custom_call_target="tpu_custom_call" | custom-call | tf_op jit(solution)/shard_map/pallas_call | solution.py:384
  51.8 1.5 %shard_map.85 = (f32[256,128]{1,0:T(8,128)}, f32[256,128]{1,0:T(8,128)}, f32[256,128]{1,0:T(8,128)}, bf16[4,2,2,2,256,128]{5,4,3,2,1,0:T(8,128)(2,1)}) custom-call(f32[256,128]{1,0:T(8,128)S(1)} %get-tuple-element.12.refs_0_, f32[256,128]{1,0:T(8,128)S(1)} %get-tuple-element.13.refs_1_, f32[256,128]{1,0:T(8,128)S(1)} %get-tuple-element.14.refs_2_, ...), custom_call_target="tpu_custom_call" | custom-call | tf_op jit(solution)/shard_map/pallas_call | solution.py:409

commit v3 on v2

--- a/solution.py
+++ b/solution.py
@@ -9,6 +9,7 @@
 
 MESH = pl.DeviceIdType.MESH
 LANES = 128
+AHEAD = 2
 VMEM_BYTES = 127 * 512 * 1024
 F32 = jnp.float32
 BF16 = jnp.bfloat16
@@ -72,9 +73,12 @@
 
     barrier = pltpu.get_barrier_semaphore()
 
-    @pl.loop(1, count)
-    def _(step):
-        pl.semaphore_signal(barrier, inc=1, device_id=((me + step) % count,), device_id_type=MESH)
+    peers = [(me + 1) % count, (me + count - 1) % count]
+    peers += [device(at(z, s, Z), y, x, core) for s in range(1, Z)]
+    peers += [device(z, at(y, o, Y), x, core) for o in range(1, Y)]
+    peers += [device(z, y, at(x, o, X), core) for o in range(1, X)]
+    for peer in peers:
+        pl.semaphore_signal(barrier, inc=1, device_id=(peer,), device_id_type=MESH)
 
     pad = rows + 8
     load_m = pltpu.make_async_copy(m_old, spans.at[0, pl.ds(pad, 2 * rows)], load_sem.at[0])
@@ -123,15 +127,24 @@
             here[which, pl.ds(row, tile)] = aligned(which, row + half)
             here[which, pl.ds(row + half, tile)] = aligned(which, row + 2 * half)
 
-    pl.semaphore_wait(barrier, count - 1)
+    pl.semaphore_wait(barrier, len(peers))
+
+    def swap_a(o, s):
+        send(grads.at[at(z, s, Z), :, at(x, o, X), 1 - core, pl.ds(0, half)],
+             mate_a.at[o, s], mate_ss_a.at[o, s], mate_rs_a.at[o, s], mate)
+
+    def swap_b(o, s):
+        send(grads.at[at(z, s, Z), at(y, o, Y), :, 1 - core, pl.ds(half, half)],
+             mate_b.at[o, s], mate_ss_b.at[o, s], mate_rs_b.at[o, s], mate)
 
     for s in order:
-        for o in list(range(1, X)) + [0]:
-            send(grads.at[at(z, s, Z), :, at(x, o, X), 1 - core, pl.ds(0, half)],
-                 mate_a.at[o, s], mate_ss_a.at[o, s], mate_rs_a.at[o, s], mate)
-        for o in list(range(1, Y)) + [0]:
-            send(grads.at[at(z, s, Z), at(y, o, Y), :, 1 - core, pl.ds(half, half)],
-                 mate_b.at[o, s], mate_ss_b.at[o, s], mate_rs_b.at[o, s], mate)
+        for o in range(1, X):
+            swap_a(o, s)
+        for o in range(1, Y):
+            swap_b(o, s)
+    for s in order:
+        swap_a(0, s)
+        swap_b(0, s)
 
     def chip_ready_a(o, s):
         loads_a[o, s].wait()
@@ -207,13 +220,15 @@
             send(send_z.at[s - 1], recv_z.at[s - 1], ss_z.at[s - 1], rs_z.at[s - 1],
                  device(at(z, s, Z), y, x, core))
 
-    for s in order:
+    for s in order[:AHEAD]:
         exchange_one(s)
     send(edge_out.at[0], edge_in.at[0], edge_ss.at[0], edge_rs.at[0], (me + count - 1) % count)
     send(edge_out.at[1], edge_in.at[1], edge_ss.at[1], edge_rs.at[1], (me + 1) % count)
     for i in range(Z + 1):
         if i < Z:
             exchange_two(order[i])
+        if AHEAD + i < Z:
+            exchange_one(order[AHEAD + i])
         if i > 0:
             exchange_three(order[i - 1])
     for s in order[:-1]:
@@ -321,9 +336,9 @@
                 send(block.at[upper], block.at[upper], dyx_ss.at[index], dyx_rs.at[index], mate)
 
     mine = full.at[z, y, x, core]
-    for s in order[:-1]:
+    ring = [0] + sorted(range(1, Z), key=lambda s: -abs(s - Z / 2))
+    for s in ring[1:]:
         send(mine, mine, gz_ss.at[s - 1], gz_rs.at[s - 1], device(at(z, s, Z), y, x, core))
-    ring = [0] + sorted(range(1, Z), key=lambda s: -abs(s - Z / 2))
     for i in range(Z + 2):
         if i < Z:
             spread(ring[i])

time: 53.4 us -> 49.2 us (0.921)
  Pallas kernels: 52.6 us -> 48.4 us
    pallas_call x1, Pallas kernels: 51.1 us -> 46.9 us  [local(): pl.pallas_call(functools.partial(kernel, dims), out_shape=(pltpu.VMEM((ro...]
where the time goes in v3:
time: 49.2 us; the launch traced here: 49.1 us
  Pallas kernels  48.4 us (98%)
  between operations  0.64 us (1%)
    pallas_call x1, Pallas kernels, local(): pl.pallas_call(functools.partial(kernel, dims), out_shape=(pltpu.VMEM((ro...  46.9 us
    pallas_call x1, Pallas kernels, local(): pl.pallas_call(publish, out_shape=(flat, flat, flat, jax.ShapeDtypeStruct...  1.49 us

profile of v3, /device:TPU:0, one launch (start us, length us, event | category | flops | bytes accessed | tf_op | source)
XLA Modules:
  0.0 49.1 jit_solution(11789869443596155941)
XLA Ops:
  0.6 46.9 %shard_map.84 = (f32[256,128]{1,0:T(8,128)S(1)}, f32[256,128]{1,0:T(8,128)S(1)}, f32[256,128]{1,0:T(8,128)S(1)}, bf16[4,2,2,2,256,128]{5,4,3,2,1,0:T(8,128)(2,1)S(1)}) custom-call(f32[4,2,2,2,256,128]{5,4,3,2,1,0:T(8,128)} %bitcast.8, f32[256,128]{1,0:T(8,128)} %bitcast.11, f32[512,128]{1,0:T(8,128)} %bitcast.9, f32[512,128]{1,0:T(8,128)} %bitcast.10, s32[33]{0:T(128)} %bounds.1), custom_call_target="tpu_custom_call" | custom-call | tf_op jit(solution)/shard_map/pallas_call | solution.py:399
  47.6 1.5 %shard_map.85 = (f32[256,128]{1,0:T(8,128)}, f32[256,128]{1,0:T(8,128)}, f32[256,128]{1,0:T(8,128)}, bf16[4,2,2,2,256,128]{5,4,3,2,1,0:T(8,128)(2,1)}) custom-call(f32[256,128]{1,0:T(8,128)S(1)} %get-tuple-element.12.refs_0_, f32[256,128]{1,0:T(8,128)S(1)} %get-tuple-element.13.refs_1_, f32[256,128]{1,0:T(8,128)S(1)} %get-tuple-element.14.refs_2_, ...), custom_call_target="tpu_custom_call" | custom-call | tf_op jit(solution)/shard_map/pallas_call | solution.py:424

commit v4 on v3

--- a/solution.py
+++ b/solution.py
@@ -10,6 +10,7 @@
 MESH = pl.DeviceIdType.MESH
 LANES = 128
 AHEAD = 2
+LAG = 3
 VMEM_BYTES = 127 * 512 * 1024
 F32 = jnp.float32
 BF16 = jnp.bfloat16
@@ -27,16 +28,16 @@
 def kernel(
     dims, grads, master, m_old, v_old, bounds,
     master_out, m_out, v_out, full,
-    own_a, own_b, mate_a, mate_b,
+    own_a, own_b, mate_a, mate_b, out_a, out_b,
     send_a1, send_b1, recv_a1, recv_b1,
     send_a2, send_b2, recv_a2, recv_b2, keep_a, keep_b,
     send_z, recv_z, gradient,
     spans, here, edge_out, edge_in, prev, weights, norm_out, norm_in,
-    load_sem, own_sem_a, own_sem_b,
+    load_sem, own_sem_a, own_sem_b, out_sem_a, out_sem_b,
     mate_ss_a, mate_rs_a, mate_ss_b, mate_rs_b,
     ss_a1, rs_a1, ss_b1, rs_b1, ss_a2, rs_a2, ss_b2, rs_b2, ss_z, rs_z,
     edge_ss, edge_rs, norm_ss, norm_rs,
-    gz_ss, gz_rs, gx_ss, gx_rs, gy_ss, gy_rs, gxy_ss, gxy_rs, gyx_ss, gyx_rs,
+    gz_ss, gz_rs, gx_ss, gx_rs, gy_ss, gy_rs, hx_ss, hx_rs, hy_ss, hy_rs, gxy_ss, gxy_rs, gyx_ss, gyx_rs,
     d_ss, d_rs, dx_ss, dx_rs, dy_ss, dy_rs, dxy_ss, dxy_rs, dyx_ss, dyx_rs,
 ):
     Z, Y, X = dims
@@ -87,8 +88,18 @@
     load_m.start()
     load_v.start()
     order = [s for s in sorted(range(1, Z), key=lambda s: abs(s - Z / 2))] + [0]
-    first, second = slice(0, half), slice(half, rows)
-    loads_a, loads_b = {}, {}
+    loads_a, loads_b, stage_a, stage_b = {}, {}, {}, {}
+    for s in order:
+        for o in range(1, X):
+            stage_a[o, s] = pltpu.make_async_copy(
+                grads.at[at(z, s, Z), :, at(x, o, X), 1 - core, pl.ds(0, half)],
+                out_a.at[o - 1, s], out_sem_a.at[o - 1, s])
+            stage_a[o, s].start()
+        for o in range(1, Y):
+            stage_b[o, s] = pltpu.make_async_copy(
+                grads.at[at(z, s, Z), at(y, o, Y), :, 1 - core, pl.ds(half, half)],
+                out_b.at[o - 1, s], out_sem_b.at[o - 1, s])
+            stage_b[o, s].start()
     for s in order:
         for o in list(range(1, X)) + [0]:
             loads_a[o, s] = pltpu.make_async_copy(
@@ -130,11 +141,15 @@
     pl.semaphore_wait(barrier, len(peers))
 
     def swap_a(o, s):
-        send(grads.at[at(z, s, Z), :, at(x, o, X), 1 - core, pl.ds(0, half)],
+        if o > 0:
+            stage_a[o, s].wait()
+        send(out_a.at[o - 1, s] if o > 0 else grads.at[at(z, s, Z), :, x, 1 - core, pl.ds(0, half)],
              mate_a.at[o, s], mate_ss_a.at[o, s], mate_rs_a.at[o, s], mate)
 
     def swap_b(o, s):
-        send(grads.at[at(z, s, Z), at(y, o, Y), :, 1 - core, pl.ds(half, half)],
+        if o > 0:
+            stage_b[o, s].wait()
+        send(out_b.at[o - 1, s] if o > 0 else grads.at[at(z, s, Z), y, :, 1 - core, pl.ds(half, half)],
              mate_b.at[o, s], mate_ss_b.at[o, s], mate_rs_b.at[o, s], mate)
 
     for s in order:
@@ -302,30 +317,40 @@
         if s > 0:
             arrived(block, gz_ss.at[s - 1], gz_rs.at[s - 1])
         for o in range(1, X):
-            send(block, block, gx_ss.at[o - 1, s], gx_rs.at[o - 1, s], device(z, y, at(x, o, X), core))
-        for o in range(1, Y):
-            send(block, block, gy_ss.at[o - 1, s], gy_rs.at[o - 1, s], device(z, at(y, o, Y), x, core))
+            send(block.at[lower], block.at[lower], gx_ss.at[o - 1, s], gx_rs.at[o - 1, s], device(z, y, at(x, o, X), core))
+        for o in range(1, Y):
+            send(block.at[upper], block.at[upper], gy_ss.at[o - 1, s], gy_rs.at[o - 1, s], device(z, at(y, o, Y), x, core))
+        for o in range(1, X):
+            send(block.at[upper], block.at[upper], hx_ss.at[o - 1, s], hx_rs.at[o - 1, s], device(z, y, at(x, o, X), core))
+        for o in range(1, Y):
+            send(block.at[lower], block.at[lower], hy_ss.at[o - 1, s], hy_rs.at[o - 1, s], device(z, at(y, o, Y), x, core))
         send(block, block, d_ss.at[s], d_rs.at[s], mate)
 
     def turn_corner(s):
         zz = at(z, Z - s, Z)
         for o in range(1, X):
             block = full.at[zz, y, at(x, X - o, X), core]
-            arrived(block, gx_ss.at[o - 1, s], gx_rs.at[o - 1, s])
+            arrived(block.at[lower], gx_ss.at[o - 1, s], gx_rs.at[o - 1, s])
             for p in range(1, Y):
                 send(block.at[lower], block.at[lower], gxy_ss.at[o - 1, p - 1, s], gxy_rs.at[o - 1, p - 1, s],
                      device(z, at(y, p, Y), x, core))
+        for p in range(1, Y):
+            block = full.at[zz, at(y, Y - p, Y), x, core]
+            arrived(block.at[upper], gy_ss.at[p - 1, s], gy_rs.at[p - 1, s])
+            for o in range(1, X):
+                send(block.at[upper], block.at[upper], gyx_ss.at[o - 1, p - 1, s], gyx_rs.at[o - 1, p - 1, s],
+                     device(z, y, at(x, o, X), core))
+
+    def finish(s):
+        zz = at(z, Z - s, Z)
+        for o in range(1, X):
+            block = full.at[zz, y, at(x, X - o, X), core]
+            arrived(block.at[upper], hx_ss.at[o - 1, s], hx_rs.at[o - 1, s])
             send(block, block, dx_ss.at[o - 1, s], dx_rs.at[o - 1, s], mate)
         for p in range(1, Y):
             block = full.at[zz, at(y, Y - p, Y), x, core]
-            arrived(block, gy_ss.at[p - 1, s], gy_rs.at[p - 1, s])
-            for o in range(1, X):
-                send(block.at[upper], block.at[upper], gyx_ss.at[o - 1, p - 1, s], gyx_rs.at[o - 1, p - 1, s],
-                     device(z, y, at(x, o, X), core))
+            arrived(block.at[lower], hy_ss.at[p - 1, s], hy_rs.at[p - 1, s])
             send(block, block, dy_ss.at[p - 1, s], dy_rs.at[p - 1, s], mate)
-
-    def finish(s):
-        zz = at(z, Z - s, Z)
         for o in range(1, X):
             for p in range(1, Y):
                 block = full.at[zz, at(y, Y - p, Y), at(x, X - o, X), core]
@@ -339,13 +364,13 @@
     ring = [0] + sorted(range(1, Z), key=lambda s: -abs(s - Z / 2))
     for s in ring[1:]:
         send(mine, mine, gz_ss.at[s - 1], gz_rs.at[s - 1], device(at(z, s, Z), y, x, core))
-    for i in range(Z + 2):
+    for i in range(Z + LAG):
         if i < Z:
             spread(ring[i])
         if 0 <= i - 1 < Z:
             turn_corner(ring[i - 1])
-        if 0 <= i - 2 < Z:
-            finish(ring[i - 2])
+        if 0 <= i - LAG < Z:
+            finish(ring[i - LAG])
     for s in range(Z):
         zz = at(z, Z - s, Z)
         arrived(full.at[zz, y, x, 1 - core], d_ss.at[s], d_rs.at[s])
@@ -376,6 +401,7 @@
     scratch = [
         vmem((X, Z, Y, half, LANES), F32), vmem((Y, Z, X, half, LANES), F32),
         vmem((X, Z, Y, half, LANES), F32), vmem((Y, Z, X, half, LANES), F32),
+        vmem((X - 1, Z, Y, half, LANES), F32), vmem((Y - 1, Z, X, half, LANES), F32),
         vmem((X - 1, Z, Y, half, LANES), BF16), vmem((Y - 1, Z, X, half, LANES), BF16),
         vmem((X - 1, Z, Y, half, LANES), BF16), vmem((Y - 1, Z, X, half, LANES), BF16),
         vmem((Y - 1, Z, half, LANES), BF16), vmem((X - 1, Z, half, LANES), BF16),
@@ -387,11 +413,12 @@
         vmem((2, 2, half, LANES), BF16), vmem((2, 2, half, LANES), BF16),
         vmem((2, rows, LANES), F32), vmem((rows, LANES), F32),
         vmem((1, LANES), F32), vmem((count, 1, LANES), F32),
-        dma((3,)), dma((X, Z)), dma((Y, Z)),
+        dma((3,)), dma((X, Z)), dma((Y, Z)), dma((X - 1, Z)), dma((Y - 1, Z)),
         *two(X, Z), *two(Y, Z),
         *two(X - 1, Z), *two(Y - 1, Z), *two(Y - 1, Z), *two(X - 1, Z), *two(Z - 1),
         *two(2), *two(count),
-        *two(Z - 1), *two(X - 1, Z), *two(Y - 1, Z), *two(X - 1, Y - 1, Z), *two(X - 1, Y - 1, Z),
+        *two(Z - 1), *two(X - 1, Z), *two(Y - 1, Z), *two(X - 1, Z), *two(Y - 1, Z),
+        *two(X - 1, Y - 1, Z), *two(X - 1, Y - 1, Z),
         *two(Z), *two(X - 1, Z), *two(Y - 1, Z), *two(X - 1, Y - 1, Z), *two(X - 1, Y - 1, Z),
     ]
     results = 12 * width + 2 * count * width

time: 49.2 us -> 47.9 us (0.974)
  Pallas kernels: 48.4 us -> 47.1 us
    pallas_call x1, Pallas kernels: 46.9 us -> 45.6 us  [local(): pl.pallas_call(functools.partial(kernel, dims), out_shape=(pltpu.VMEM((ro...]
where the time goes in v4:
time: 47.9 us; the launch traced here: 47.7 us
  Pallas kernels  47.1 us (98%)
  between operations  0.64 us (1%)
    pallas_call x1, Pallas kernels, local(): pl.pallas_call(functools.partial(kernel, dims), out_shape=(pltpu.VMEM((ro...  45.6 us
    pallas_call x1, Pallas kernels, local(): pl.pallas_call(publish, out_shape=(flat, flat, flat, jax.ShapeDtypeStruct...  1.49 us

profile of v4, /device:TPU:0, one launch (start us, length us, event | category | flops | bytes accessed | tf_op | source)
XLA Modules:
  0.0 47.7 jit_solution(2482187948049588989)
XLA Ops:
  0.6 45.6 %shard_map.84 = (f32[256,128]{1,0:T(8,128)S(1)}, f32[256,128]{1,0:T(8,128)S(1)}, f32[256,128]{1,0:T(8,128)S(1)}, bf16[4,2,2,2,256,128]{5,4,3,2,1,0:T(8,128)(2,1)S(1)}) custom-call(f32[4,2,2,2,256,128]{5,4,3,2,1,0:T(8,128)} %bitcast.8, f32[256,128]{1,0:T(8,128)} %bitcast.11, f32[512,128]{1,0:T(8,128)} %bitcast.9, f32[512,128]{1,0:T(8,128)} %bitcast.10, s32[33]{0:T(128)} %bounds.1), custom_call_target="tpu_custom_call" | custom-call | tf_op jit(solution)/shard_map/pallas_call | solution.py:426
  46.2 1.5 %shard_map.85 = (f32[256,128]{1,0:T(8,128)}, f32[256,128]{1,0:T(8,128)}, f32[256,128]{1,0:T(8,128)}, bf16[4,2,2,2,256,128]{5,4,3,2,1,0:T(8,128)(2,1)}) custom-call(f32[256,128]{1,0:T(8,128)S(1)} %get-tuple-element.12.refs_0_, f32[256,128]{1,0:T(8,128)S(1)} %get-tuple-element.13.refs_1_, f32[256,128]{1,0:T(8,128)S(1)} %get-tuple-element.14.refs_2_, ...), custom_call_target="tpu_custom_call" | custom-call | tf_op jit(solution)/shard_map/pallas_call | solution.py:451
